TPU v7x, 256 devices: a whole 4x4x8 slice. The times are simulated.
256 devices in a mesh: cells: 32 (over z, x), genes: 8 (over y, core).
Axes of the slice: x: 4, y: 4, z: 8, core: 2. Of those that a mesh axis runs over, the one named last changes fastest.
Arguments:
- expression: bfloat16 [131072, 4096], P('cells', 'genes'), may hold values from -200 to 200
- labels: int32 [131072], P('cells'), may hold values from 0 to 199, as said below
- loadings: bfloat16 [4096, 50], P('genes'), may hold values from -0.09375 to 0.09375
Outputs:
- adjusted: bfloat16 [131072, 4096], P('cells', 'genes')
- scores: float32 [131072, 50], P('cells')
Inputs may be any that keep to these rules, and one draw needn't show every extreme that they name: `labels`: every batch has two or more cells.
All inputs are finite; a program needn't handle non-finite values.
Results may differ from a plain program's by a relative error of at most 0.0029.
Values sent between devices are 32-bit elements; how exact they have to be, the bound alone decides.
A program may use at most 64 MiB of HBM per device.

v0:
```python
import math

import jax
import jax.numpy as jnp
from jax import lax
from jax.sharding import PartitionSpec as P

GENES = 4096
BATCHES = 200
SWEEPS = 10


def padded_to(lines, length):
    spare = -len(lines) % length
    return jnp.pad(lines, [(0, spare)] + [(0, 0)] * (lines.ndim - 1))


def sent_to_all(value, axis):
    length = lax.axis_size(axis)
    return lax.all_to_all(
        jnp.broadcast_to(value[None], (length, *value.shape)), axis, 0, 0, tiled=True
    )


def laid_out(blocks, dim):
    blocks = jnp.moveaxis(blocks, 0, dim)
    dims = blocks.shape
    return blocks.reshape(*dims[:dim], dims[dim] * dims[dim + 1], *dims[dim + 2 :])


def collect(value, axis, dim):
    blocks = sent_to_all(value, axis)
    return laid_out(blocks, dim)


def split_up(value, dim, length):
    before, after = (value.shape[:dim], value.shape[dim + 1 :])
    return jnp.moveaxis(value.reshape(*before, length, -1, *after), dim, 0)


def sum_at_owner(value, axis, dim):
    length = lax.axis_size(axis)
    blocks = lax.all_to_all(split_up(value, dim, length), axis, 0, 0, tiled=True)
    return jnp.sum(blocks, axis=0)


def sum_by_parts(value, axes):
    padded = padded_to(value, lax.axis_size(axes))
    whole = collect(sum_at_owner(padded, axes, 0), axes, 0)
    return lax.slice_in_dim(whole, 0, len(value)).reshape(value.shape)


def together(arrays, axis):
    ends = [0]
    for a in arrays:
        ends.append(ends[-1] + a.size)
    running = sum_by_parts(jnp.concatenate([a.ravel() for a in arrays]), axis)
    return tuple((running[b:e].reshape(a.shape) for a, b, e in zip(arrays, ends, ends[1:])))


def taken_together(value, axis):
    everything = sent_to_all(value, axis)
    return jnp.sum(everything, axis=0)


def sum_by_parts_2(value, axis):
    lines = value.reshape(-1, *value.shape[1:][-1:])
    own = lax.psum_scatter(
        padded_to(lines, lax.axis_size(axis)), axis, scatter_dimension=0, tiled=True
    )
    whole = lax.all_gather(own, axis).reshape(-1, *lines.shape[1:])
    return lax.slice_in_dim(whole, 0, len(lines)).reshape(value.shape)


def batch_moments(sum_one, sum_two, counts, total_cells):
    grand = jnp.sum(sum_one, axis=0) / total_cells
    within = sum_two - sum_one * sum_one / counts[:, None]
    pooled = jnp.sum(within, axis=0) / total_cells + 1e-06
    gene_sd = jnp.sqrt(pooled)
    gamma_hat = (sum_one / counts[:, None] - grand[None, :]) / gene_sd[None, :]
    delta_hat = within / ((counts[:, None] - 1.0) * pooled[None, :])
    return (grand, gene_sd, gamma_hat, delta_hat)


def gene_terms(gamma_hat, delta_hat):
    return (
        jnp.sum(gamma_hat, axis=1),
        jnp.sum(gamma_hat * gamma_hat, axis=1),
        jnp.sum(delta_hat, axis=1),
        jnp.sum(delta_hat * delta_hat, axis=1),
    )


def shrink(gamma_hat, delta_hat, counts, spread):
    sum_gamma, sum_gamma_sq, sum_delta, sum_delta_sq = spread
    gamma_bar = sum_gamma / GENES
    tau_sq = (sum_gamma_sq - GENES * gamma_bar * gamma_bar) / (GENES - 1)
    delta_mean = sum_delta / GENES
    delta_var = (sum_delta_sq - GENES * delta_mean * delta_mean) / (GENES - 1) + 1e-06
    a_prior = (2.0 * delta_var + delta_mean * delta_mean) / delta_var
    b_prior = (delta_mean * delta_var + delta_mean**3) / delta_var
    weight = counts[:, None]

    def sweep(sweep_index, state):
        gamma_now, delta_now = state
        gamma_next = (weight * tau_sq[:, None] * gamma_hat + delta_now * gamma_bar[:, None]) / (
            weight * tau_sq[:, None] + delta_now
        )
        sum_sq = (weight - 1.0) * delta_hat + weight * (gamma_hat - gamma_next) ** 2
        delta_next = (0.5 * sum_sq + b_prior[:, None]) / (0.5 * weight + a_prior[:, None] - 1.0)
        return (gamma_next, delta_next)

    gamma_star, delta_star = lax.fori_loop(0, SWEEPS, sweep, (gamma_hat, delta_hat))
    return (gamma_star, 1.0 / jnp.sqrt(delta_star))


def split_three(initial):
    upper_part = lax.optimization_barrier(initial.astype(jnp.bfloat16))
    remainder = initial - upper_part.astype(jnp.float32)
    middle_part = lax.optimization_barrier(remainder.astype(jnp.bfloat16))
    lower_part = (remainder - middle_part.astype(jnp.float32)).astype(jnp.bfloat16)
    return (upper_part, middle_part, lower_part)


def body(expression, labels, loadings):
    cell_rows, gene_cols = expression.shape
    block_rows = math.gcd(cell_rows, 1024)
    block_count = cell_rows // block_rows
    indices = jnp.arange(block_count, dtype=jnp.int32)
    batch_ids = jnp.arange(BATCHES, dtype=jnp.int32)
    total_cells = cell_rows * lax.axis_size("cells")

    def members_of(start):
        local_labels = lax.dynamic_slice_in_dim(labels, start, block_rows, 0)
        return (batch_ids[:, None] == local_labels[None, :]).astype(jnp.bfloat16)

    def accumulate(totals, block_index):
        start = block_index * block_rows
        values = lax.dynamic_slice_in_dim(expression, start, block_rows, 0)
        widened = values.astype(jnp.float32)
        square_upper, square_middle, square_lower = split_three(widened * widened)
        stacked = jnp.concatenate([values, square_upper, square_middle, square_lower], axis=1)
        members = members_of(start)
        product = jnp.dot(members, stacked, preferred_element_type=jnp.float32)
        first = product[:, :gene_cols]
        second = (
            product[:, gene_cols : 2 * gene_cols]
            + product[:, 2 * gene_cols : 3 * gene_cols]
            + product[:, 3 * gene_cols :]
        )
        number = jnp.sum(members.astype(jnp.float32), axis=1)
        return ((totals[0] + first, totals[1] + second, totals[2] + number), None)

    zeros_table = jnp.zeros((BATCHES, gene_cols), jnp.float32)
    (sum_one, sum_two, counts), unused = lax.scan(
        accumulate, (zeros_table, zeros_table, jnp.zeros((BATCHES,), jnp.float32)), indices
    )
    sum_one, sum_two, counts = together((sum_one, sum_two, counts), "cells")
    grand, gene_sd, gamma_hat, delta_hat = batch_moments(sum_one, sum_two, counts, total_cells)
    spread = jax.tree.map(
        lambda part: taken_together(part, "genes"), gene_terms(gamma_hat, delta_hat)
    )
    gamma_star, scale_star = shrink(gamma_hat, delta_hat, counts, spread)
    table_parts = split_three(jnp.concatenate([gamma_star, scale_star], axis=1))

    def adjust(block_index):
        start = block_index * block_rows
        values = lax.dynamic_slice_in_dim(expression, start, block_rows, 0).astype(jnp.float32)
        members = members_of(start)
        looked = lax.dot_general(
            members, table_parts[0], (((0,), (0,)), ((), ())), preferred_element_type=jnp.float32
        )
        looked = looked + lax.dot_general(
            members, table_parts[1], (((0,), (0,)), ((), ())), preferred_element_type=jnp.float32
        )
        looked = looked + lax.dot_general(
            members, table_parts[2], (((0,), (0,)), ((), ())), preferred_element_type=jnp.float32
        )
        shifted = (values - grand[None, :]) / gene_sd[None, :]
        standard = (shifted - looked[:, :gene_cols]) * looked[:, gene_cols:]
        adjusted = (gene_sd[None, :] * standard + grand[None, :]).astype(jnp.bfloat16)
        standard_low = standard.astype(jnp.bfloat16)
        partial_value = jnp.dot(standard_low, loadings, preferred_element_type=jnp.float32)
        return (adjusted, partial_value)

    adjusted, partial_value = lax.map(adjust, indices)
    adjusted = adjusted.reshape(cell_rows, gene_cols)
    partial_value = partial_value.reshape(cell_rows, loadings.shape[1])
    scores = sum_by_parts_2(partial_value, "genes")
    return (adjusted, scores)


def solution(mesh):
    placed = (P("cells", "genes"), P("cells"), P("genes", None))
    return jax.shard_map(
        body,
        mesh=mesh,
        in_specs=placed,
        out_specs=(P("cells", "genes"), P("cells", None)),
        check_vma=False,
    )
```

profile of v0, /device:TPU:1, one launch (start us, length us, event | category | flops | bytes accessed | tf_op | source)
XLA Modules:
  0.0 250.4 jit_solution(15040133324050709078)
XLA Ops:
  7.2 23.5 %while.45 = (s32[]{:T(128)}, f32[200,512]{1,0:T(8,128)S(1)}, f32[200,512]{1,0:T(8,128)S(1)}, f32[200]{0:T(256)S(1)}, s32[4]{0:T(128)S(1)}, /*index=5*/s32[4096]{...) while((s32[]{:T(128)}, f32[200,512]{1,0:T(8,128)S(1)}, ...), condition=%wide.region_2.3_spmd.clone, body=%wide.region_0.2_spmd.clone.sunk | while | flops 865140928 | bytes 19615032 | solution.py:155
  8.5 1.5 fusion.64
  11.5 1.1 fusion.66
  14.3 1.5 fusion.64
  17.3 1.1 fusion.66
  20.2 1.5 fusion.64
  23.2 1.1 fusion.66
  26.1 1.5 fusion.64
  29.1 1.1 fusion.66
  31.0 1.1 all_to_all.26
  32.1 33.6 %all_to_all.39 = f32[32,1,6407]{2,1,0:T(1,128)S(1)} all-to-all(f32[32,1,6407]{2,1,0:T(1,128)S(1)} %all_to_all.26), channel_id=1, replica_groups=mesh['cells'=32,'genes'=8] {'cells'}, dimensions={0} | all-to-all | bytes 1640192 | tf_op jit(solution)/shard_map/all_to_all | solution.py:43
  66.6 26.4 %all_to_all.40 = f32[32,1,6407]{2,1,0:T(1,128)S(1)} all-to-all(f32[32,1,6407]{2,1,0:T(1,128)S(1)} %broadcast_in_dim.32), channel_id=1, replica_groups=mesh['cells'=32,'genes'=8] {'cells'}, dimensions={0} | all-to-all | bytes 1640192 | tf_op jit(solution)/shard_map/all_to_all | solution.py:20
  93.0 2.0 reduce.5
  96.1 13.1 %all_to_all.41 = f32[8,1,200]{2,1,0:T(1,128)S(1)} all-to-all(f32[8,1,200]{2,1,0:T(1,128)S(1)} %broadcast_in_dim.33), channel_id=1, replica_groups=mesh['cells'=32,'genes'=8] {'genes'}, dimensions={0} | all-to-all | bytes 12800 | tf_op jit(solution)/shard_map/all_to_all | solution.py:20
  109.8 3.9 %all-to-all-start.3 = ((f32[8,1,200]{2,1,0:T(1,128)}), f32[8,1,200]{2,1,0:T(1,128)S(1)}, u32[]{:S(2)}, u32[]{:S(2)}) async-start(f32[8,1,200]{2,1,0:T(1,128)} %broadcast_in_dim.34), calls=%async_computation.3 | async-start | bytes 16384 | tf_op jit(solution)/shard_map/all_to_all | solution.py:20
  113.8 4.6 %all-to-all-done.3 = f32[8,1,200]{2,1,0:T(1,128)S(1)} async-done(((f32[8,1,200]{2,1,0:T(1,128)}), f32[8,1,200]{2,1,0:T(1,128)S(1)}, u32[]{:S(2)}, u32[]{:S(2)}) %all-to-all-start.3) | async-done | bytes 6432 | tf_op jit(solution)/shard_map/all_to_all | solution.py:20
  118.8 7.7 %all_to_all.42 = f32[8,1,200]{2,1,0:T(1,128)S(1)} all-to-all(f32[8,1,200]{2,1,0:T(1,128)S(1)} %broadcast_in_dim.36), channel_id=1, replica_groups=mesh['cells'=32,'genes'=8] {'genes'}, dimensions={0} | all-to-all | bytes 12800 | tf_op jit(solution)/shard_map/all_to_all | solution.py:20
  127.0 3.9 %all-to-all-start.5 = ((f32[8,1,200]{2,1,0:T(1,128)}), f32[8,1,200]{2,1,0:T(1,128)S(1)}, u32[]{:S(2)}, u32[]{:S(2)}) async-start(f32[8,1,200]{2,1,0:T(1,128)} %broadcast_in_dim.37), calls=%async_computation.5 | async-start | bytes 16384 | tf_op jit(solution)/shard_map/all_to_all | solution.py:20
  131.8 3.8 %all-to-all-done.5 = f32[8,1,200]{2,1,0:T(1,128)S(1)} async-done(((f32[8,1,200]{2,1,0:T(1,128)}), f32[8,1,200]{2,1,0:T(1,128)S(1)}, u32[]{:S(2)}, u32[]{:S(2)}) %all-to-all-start.5) | async-done | bytes 6432 | tf_op jit(solution)/shard_map/all_to_all | solution.py:20
  135.7 10.2 %while.43 = (s32[]{:T(128)}, f32[200,512]{1,0:T(8,128)}, f32[200,512]{1,0:T(8,128)S(1)}, f32[200,1]{0,1:T(1,128)S(1)}, f32[200,512]{1,0:T(8,128)S(1)}, /*index=5...) while((s32[]{:T(128)}, f32[200,512]{1,0:T(8,128)}, ...), condition=%wide.region_15.16_spmd, body=%wide.region_14.15_spmd.sunk | while | flops 1332002 | bytes 2056109 | solution.py:113
  135.7 1.0 add_divide_fusion.5
  136.7 1.0 add_divide_fusion.5
  137.7 1.0 add_divide_fusion.5
  138.7 1.0 add_divide_fusion.5
  139.7 1.0 add_divide_fusion.5
  140.8 1.0 add_divide_fusion.5
  141.8 1.0 add_divide_fusion.5
  142.8 1.0 add_divide_fusion.5
  143.8 1.0 add_divide_fusion.5
  144.8 1.0 add_divide_fusion.5
  145.9 1.1 fusion.26
  147.0 1.1 fusion.27
  148.1 1.2 subtract_convert_fusion.1
  149.3 48.0 %while.44 = (s32[]{:T(128)}, bf16[4,1024,512]{2,1,0:T(8,128)(2,1)}, f32[4,1024,50]{1,0,2:T(4,128)S(1)}, f32[512]{0:T(512)S(1)}, s32[4]{0:T(128)S(1)}, /*index=5*...) while((s32[]{:T(128)}, bf16[4,1024,512]{2,1,0:T(8,128)(2,1)}, ...), condition=%wide.region_17.18_spmd.clone, body=%wide.region_16.17_spmd.clone.sunk | while | flops 1318150144 | bytes 31689436 | solution.py:186
  152.7 0.8 add_add_fusion.3
  153.5 2.9 %fusion.62 = (bf16[4,1024,512]{2,1,0:T(8,128)(2,1)}, bf16[1024,512]{1,0:T(8,128)(2,1)S(1)}) fusion(bf16[4,1024,512]{2,1,0:T(8,128)(2,1)} %get-tuple-element.691, s32[]{:T(128)} %get-tuple-element.690, f32[512]{0:T(512)S(1)} %get-tuple-element.712, f32[512]{0:T(512)S(1)} %get-tuple-element.709, f32[1024,1024]{1,0:T(8,128)S(1)} %add_add_fusion.3, ...), kind=kLoop, calls=%fused_computation.12.clone.1 | loop fusion | flops 4718592 | bytes 7344644 | tf_op jit(solution)/shard_map/while/body/jit(dynamic_update_index_in_dim)/dynamic_update_slice | solution.py:186
  157.1 4.2 %dynamic_update_slice.14 = f32[4,1024,50]{1,0,2:T(4,128)S(1)} dynamic-update-slice(f32[4,1024,50]{1,0,2:T(4,128)S(1)} %get-tuple-element.692, f32[1,1024,50]{1,0,2:T(1,128)S(1)} %copy.36, s32[]{:T(128)} %get-tuple-element.690, s32[]{:T(128)} %constant.77.clone.1..sunk, s32[]{:T(128)} %constant.77.clone.1..sunk) | dynamic-update-slice | bytes 409604 | tf_op jit(solution)/shard_map/while/body/jit(dynamic_update_index_in_dim)/dynamic_update_slice | solution.py:186
  165.5 2.9 %fusion.62 = (bf16[4,1024,512]{2,1,0:T(8,128)(2,1)}, bf16[1024,512]{1,0:T(8,128)(2,1)S(1)}) fusion(bf16[4,1024,512]{2,1,0:T(8,128)(2,1)} %get-tuple-element.691, s32[]{:T(128)} %get-tuple-element.690, f32[512]{0:T(512)S(1)} %get-tuple-element.712, f32[512]{0:T(512)S(1)} %get-tuple-element.709, f32[1024,1024]{1,0:T(8,128)S(1)} %add_add_fusion.3, ...), kind=kLoop, calls=%fused_computation.12.clone.1 | loop fusion | flops 4718592 | bytes 7344644 | tf_op jit(solution)/shard_map/while/body/jit(dynamic_update_index_in_dim)/dynamic_update_slice | solution.py:186
  169.1 4.2 %dynamic_update_slice.14 = f32[4,1024,50]{1,0,2:T(4,128)S(1)} dynamic-update-slice(f32[4,1024,50]{1,0,2:T(4,128)S(1)} %get-tuple-element.692, f32[1,1024,50]{1,0,2:T(1,128)S(1)} %copy.36, s32[]{:T(128)} %get-tuple-element.690, s32[]{:T(128)} %constant.77.clone.1..sunk, s32[]{:T(128)} %constant.77.clone.1..sunk) | dynamic-update-slice | bytes 409604 | tf_op jit(solution)/shard_map/while/body/jit(dynamic_update_index_in_dim)/dynamic_update_slice | solution.py:186
  177.5 2.9 %fusion.62 = (bf16[4,1024,512]{2,1,0:T(8,128)(2,1)}, bf16[1024,512]{1,0:T(8,128)(2,1)S(1)}) fusion(bf16[4,1024,512]{2,1,0:T(8,128)(2,1)} %get-tuple-element.691, s32[]{:T(128)} %get-tuple-element.690, f32[512]{0:T(512)S(1)} %get-tuple-element.712, f32[512]{0:T(512)S(1)} %get-tuple-element.709, f32[1024,1024]{1,0:T(8,128)S(1)} %add_add_fusion.3, ...), kind=kLoop, calls=%fused_computation.12.clone.1 | loop fusion | flops 4718592 | bytes 7344644 | tf_op jit(solution)/shard_map/while/body/jit(dynamic_update_index_in_dim)/dynamic_update_slice | solution.py:186
  181.1 4.2 %dynamic_update_slice.14 = f32[4,1024,50]{1,0,2:T(4,128)S(1)} dynamic-update-slice(f32[4,1024,50]{1,0,2:T(4,128)S(1)} %get-tuple-element.692, f32[1,1024,50]{1,0,2:T(1,128)S(1)} %copy.36, s32[]{:T(128)} %get-tuple-element.690, s32[]{:T(128)} %constant.77.clone.1..sunk, s32[]{:T(128)} %constant.77.clone.1..sunk) | dynamic-update-slice | bytes 409604 | tf_op jit(solution)/shard_map/while/body/jit(dynamic_update_index_in_dim)/dynamic_update_slice | solution.py:186
  188.8 0.8 add_add_fusion.3
  189.5 2.9 %fusion.62 = (bf16[4,1024,512]{2,1,0:T(8,128)(2,1)}, bf16[1024,512]{1,0:T(8,128)(2,1)S(1)}) fusion(bf16[4,1024,512]{2,1,0:T(8,128)(2,1)} %get-tuple-element.691, s32[]{:T(128)} %get-tuple-element.690, f32[512]{0:T(512)S(1)} %get-tuple-element.712, f32[512]{0:T(512)S(1)} %get-tuple-element.709, f32[1024,1024]{1,0:T(8,128)S(1)} %add_add_fusion.3, ...), kind=kLoop, calls=%fused_computation.12.clone.1 | loop fusion | flops 4718592 | bytes 7344644 | tf_op jit(solution)/shard_map/while/body/jit(dynamic_update_index_in_dim)/dynamic_update_slice | solution.py:186
  193.1 4.2 %dynamic_update_slice.14 = f32[4,1024,50]{1,0,2:T(4,128)S(1)} dynamic-update-slice(f32[4,1024,50]{1,0,2:T(4,128)S(1)} %get-tuple-element.692, f32[1,1024,50]{1,0,2:T(1,128)S(1)} %copy.36, s32[]{:T(128)} %get-tuple-element.690, s32[]{:T(128)} %constant.77.clone.1..sunk, s32[]{:T(128)} %constant.77.clone.1..sunk) | dynamic-update-slice | bytes 409604 | tf_op jit(solution)/shard_map/while/body/jit(dynamic_update_index_in_dim)/dynamic_update_slice | solution.py:186
  197.5 1.5 copy.34
  198.9 27.2 %reduce-scatter.2.cloned.1.call-done = f32[512,50]{0,1:T(8,128)} async-done(((f32[4096,50]{0,1:T(8,128)}), f32[512,50]{0,1:T(8,128)}) %reduce-scatter.2.cloned.1.call-update) | async-done | bytes 102416 | tf_op jit(solution)/shard_map/reduce_scatter | solution.py:68
  226.1 16.5 %all-gather = f32[4096,50]{0,1:T(8,128)S(1)} all-gather(f32[512,50]{0,1:T(8,128)} %reduce-scatter.2.cloned.1.call-done), channel_id=2, replica_groups=mesh['cells'=32,'genes'=8] {'genes'}, dimensions={0}, use_global_device_ids=true | all-gather | bytes 921600 | tf_op jit(solution)/shard_map/all_gather | solution.py:71
  242.6 0.9 copy.70
  (103 shorter events, 30.9 us)
Async XLA Ops:
  109.8 8.6 %all-to-all-start.3 = ((f32[8,1,200]{2,1,0:T(1,128)}), f32[8,1,200]{2,1,0:T(1,128)S(1)}, u32[]{:S(2)}, u32[]{:S(2)}) async-start(f32[8,1,200]{2,1,0:T(1,128)} %broadcast_in_dim.34), calls=%async_computation.3 | async-start | bytes 16384 | tf_op jit(solution)/shard_map/all_to_all | solution.py:20
  127.0 8.6 %all-to-all-start.5 = ((f32[8,1,200]{2,1,0:T(1,128)}), f32[8,1,200]{2,1,0:T(1,128)S(1)}, u32[]{:S(2)}, u32[]{:S(2)}) async-start(f32[8,1,200]{2,1,0:T(1,128)} %broadcast_in_dim.37), calls=%async_computation.5 | async-start | bytes 16384 | tf_op jit(solution)/shard_map/all_to_all | solution.py:20
  131.0 95.1 %reduce-scatter.2.cloned.1.call-start = ((), (), s32[]{:S(2)}) async-start(), calls=%async_computation.7 | async-start | bytes 1032192 | tf_op jit(solution)/shard_map/reduce_scatter | solution.py:68
  145.8 3.4 %copy-start = (bf16[512,50]{0,1:T(8,128)(2,1)S(1)}, bf16[512,50]{0,1:T(8,128)(2,1)}, u32[]{:S(2)}) copy-start(bf16[512,50]{0,1:T(8,128)(2,1)} %param.11) | copy-start | bytes 153604
Sparse Core Ops, SparseCore 0:
  199.0 26.9 reduce-scatter.1
where the time goes:
time: 251 us; the launch traced here: 250 us
  blocking collectives  97.3 us (39%)
  other arithmetic  39.6 us (16%)
  waiting for transfers between devices  35.6 us (14%)
  local copies, waits for them, and re-layouts  34.8 us (14%)
  matrix products  15.2 us (6%)
  between operations  14.2 us (6%)
  starting transfers between devices  7.87 us (3%)
  loops' own time  5.7 us (2%)
    all_to_all x3, blocking collectives, sent_to_all(): lax.all_to_all(jnp.broadcast_to(value[None], (length, *value.shape)), axi...  47.2 us
    all_to_all x1, blocking collectives, sum_at_owner(): lax.all_to_all(split_up(value, dim, length), axis, 0, 0, tiled=True)  33.6 us
    reduce_scatter x1, waiting for transfers between devices, sum_by_parts_2(): lax.psum_scatter(padded_to(lines, lax.axis_size(axis)), axis, scatter_dim...  27.2 us
    dynamic_update_slice x8, local copies, waits for them, and re-layouts, body(): adjusted, partial_value = lax.map(adjust, indices)  17.6 us
    all_gather x1, blocking collectives, sum_by_parts_2(): whole = lax.all_gather(own, axis).reshape(-1, *lines.shape[1:])  16.5 us
    dynamic_update_slice x4, other arithmetic, body(): adjusted, partial_value = lax.map(adjust, indices)  11.5 us
    div x10, other arithmetic, sweep(): (0.5 * sum_sq + b_prior[:, None]) / (0.5 * weight + a_prior[:, None] - 1.0)  10.1 us
    all_to_all x2, waiting for transfers between devices, sent_to_all(): lax.all_to_all(jnp.broadcast_to(value[None], (length, *value.shape)), axi...  8.43 us
  transfers between devices with their start and end apart: 3, of which 3 were waited for; matrix products, arithmetic and copies ran while one was open for 0% of the time, Pallas kernels for 0%

commit v1 on v0

v1 whole, which is shorter than its diff:
```python
import functools

import jax
import jax.numpy as jnp
from jax import lax
from jax.experimental import pallas as pl
from jax.experimental.pallas import tpu as pltpu
from jax.sharding import PartitionSpec as P

MESH = pl.DeviceIdType.MESH
GENES = 4096
BATCHES = 200
CELLS = 131072
SWEEPS = 10
COMPONENTS = 50

NZ, NX, NY = 8, 4, 4
ROWS, COLS = 4096, 512
LANES = 128
GROUPS = COLS // LANES
PART = 56
HALF = 32
STACK = NZ * PART
COUNT_ROW = 2 * BATCHES
PAD = 256
READ = 1024
STEP = 512
CHUNK_TOP = 32

f32, bf16, i32 = jnp.float32, jnp.bfloat16, jnp.int32
NT = (((1,), (1,)), ((), ()))


def z_offset(k):
    size = 4 - (k + 1) // 2
    return (size if k % 2 else NZ - size) % NZ


def remote(src, dst, send, recv, cells, genes):
    return pltpu.make_async_remote_copy(
        src_ref=src,
        dst_ref=dst,
        send_sem=send,
        recv_sem=recv,
        device_id={"cells": cells, "genes": genes},
        device_id_type=MESH,
    )


def kernel(
    labels,
    x_hbm,
    loadings_t,
    adjusted_hbm,
    scores_hbm,
    xv,
    outv,
    onehot,
    acc_one,
    acc_two,
    acc_count,
    sums,
    via_left,
    via_right,
    from_left,
    from_right,
    owned,
    from_z,
    table,
    terms,
    terms_y,
    terms_x,
    cols,
    gene_rows,
    wide,
    pair,
    part,
    part_recv,
    role,
    y_via_left,
    y_via_right,
    y_from_left,
    y_from_right,
    final,
    x_sem,
    out_sem,
    fin_sem,
    rs_send,
    rs_recv,
    z_send,
    z_recv,
    g_send,
    g_recv,
    ag_send,
    ag_recv,
    t_send,
    t_recv,
    d_send,
    d_recv,
    y_send,
    y_recv,
):
    me_c = lax.axis_index("cells")
    me_g = lax.axis_index("genes")
    mz, mx = lax.div(me_c, NX), lax.rem(me_c, NX)
    my, mh = lax.div(me_g, 2), lax.rem(me_g, 2)
    x_right, x_left, x_opp = (lax.rem(mx + d, NX) for d in (1, 3, 2))
    y_right, y_left, y_opp = (lax.rem(my + d, NY) for d in (1, 3, 2))

    def cell(z, x):
        return z * NX + x

    right, left = cell(mz, x_right), cell(mz, x_left)
    barrier = pltpu.get_barrier_semaphore()

    def greet(c, g):
        pl.semaphore_signal(
            barrier, inc=1, device_id={"cells": c, "genes": g}, device_id_type=MESH
        )

    for r in range(1, NX):
        greet(cell(mz, lax.rem(mx + r, NX)), me_g)
    for r in range(1, NZ):
        greet(cell(lax.rem(mz + r, NZ), mx), me_g)
    for r in range(1, 2 * NY):
        greet(me_c, lax.rem(me_g + r, 2 * NY))

    def x_copy(i):
        rows = pl.ds(pl.multiple_of(i * READ, READ), READ)
        return pltpu.make_async_copy(x_hbm.at[rows, :], xv.at[rows, :], x_sem.at[i])

    for i in range(ROWS // READ):
        x_copy(i).start()
    acc_one[...] = jnp.zeros_like(acc_one)
    acc_two[...] = jnp.zeros_like(acc_two)
    acc_count[...] = jnp.zeros_like(acc_count)

    def first_pass(i, carry):
        tile = labels[pl.ds(pl.multiple_of(i * 8, 8), 8), :]
        ids = lax.broadcasted_iota(i32, (208, LANES), 0)
        members = jnp.concatenate(
            [jnp.where(ids == tile[j : j + 1, :], 1.0, 0.0).astype(bf16) for j in range(8)], axis=1
        )
        x_copy(i).wait()
        values = xv[pl.ds(pl.multiple_of(i * READ, READ), READ), :]
        widened = values.astype(f32)
        square = widened * widened
        upper = square.astype(bf16)
        lower = (square - upper.astype(f32)).astype(bf16)
        acc_one[...] += jnp.dot(members, values, preferred_element_type=f32)
        acc_two[...] += jnp.dot(members, upper, preferred_element_type=f32) + jnp.dot(
            members, lower, preferred_element_type=f32
        )
        ones = jnp.ones((8, READ), bf16)
        acc_count[:, :208] += lax.dot_general(ones, members, NT, preferred_element_type=f32)
        return carry

    lax.fori_loop(0, ROWS // READ, first_pass, 0)
    sub = lax.broadcasted_iota(i32, (8, LANES), 0)
    count_tile = jnp.where(sub == 0, acc_count[:, :LANES], acc_count[:, LANES:])
    for g in range(GROUPS):
        lanes = slice(g * LANES, (g + 1) * LANES)
        sums[g, 0:BATCHES, :] = acc_one[0:BATCHES, lanes]
        sums[g, BATCHES:COUNT_ROW, :] = acc_two[0:BATCHES, lanes]
        sums[g, COUNT_ROW : COUNT_ROW + 8, :] = count_tile
        sums[g, COUNT_ROW + 8 :, :] = jnp.zeros((STACK - COUNT_ROW - 8, LANES), f32)

    pl.semaphore_wait(barrier, NX - 1 + NZ - 1 + 2 * NY - 1)

    def z_of(k):
        return lax.rem(mz + z_offset(k), NZ)

    def top(z):
        return pl.ds(pl.multiple_of(z * PART, 8), HALF)

    def low(z):
        return pl.ds(pl.multiple_of(z * PART + HALF, 8), PART - HALF)

    def whole(z):
        return pl.ds(pl.multiple_of(z * PART, 8), PART)

    def rs(kind, k):
        z = z_of(k)
        src, dst, to = (
            (sums.at[x_opp, top(z)], via_left.at[k], right),
            (sums.at[x_opp, low(z)], via_right.at[k], left),
            (sums.at[x_right, low(z)], from_left.at[k, HALF:PART], right),
            (sums.at[x_left, top(z)], from_right.at[k, 0:HALF], left),
            (sums.at[x_right, top(z)], from_left.at[k, 0:HALF], right),
            (sums.at[x_left, low(z)], from_right.at[k, HALF:PART], left),
        )[kind]
        return remote(src, dst, rs_send.at[kind, k], rs_recv.at[kind, k], to, me_g)

    def z_copy(k):
        return remote(owned.at[k], from_z.at[k], z_send.at[k], z_recv.at[k], cell(z_of(k), mx), me_g)

    def issue(k):
        for kind in range(4):
            rs(kind, k).start()

    def merge(k):
        z = z_of(k)
        rs(0, k).wait_recv()
        sums[x_right, top(z)] += via_left[k]
        rs(4, k).start()
        rs(1, k).wait_recv()
        sums[x_left, low(z)] += via_right[k]
        rs(5, k).start()

    def finish(k):
        for kind in range(2, 6):
            rs(kind, k).wait_recv()
        owned[k] = sums[mx, whole(z_of(k))] + from_left[k] + from_right[k]
        if k < NZ - 1:
            z_copy(k).start()

    issue(0)
    issue(1)

    def spread_labels(i, carry):
        wide_labels = jnp.broadcast_to(labels[pl.ds(i, 1), :].astype(f32), (LANES, LANES)).T
        ids = lax.broadcasted_iota(i32, (LANES, LANES), 1).astype(f32)
        rows = pl.ds(pl.multiple_of(i * LANES, LANES), LANES)
        onehot[rows, 0:LANES] = jnp.where(wide_labels == ids, 1.0, 0.0).astype(bf16)
        onehot[rows, LANES:PAD] = jnp.where(wide_labels == ids + LANES, 1.0, 0.0).astype(bf16)
        return carry

    lax.fori_loop(0, ROWS // LANES, spread_labels, 0)
    for k in range(NZ):
        merge(k)
        if k + 2 < NZ:
            issue(k + 2)
        if k >= 1:
            finish(k - 1)
    finish(NZ - 1)
    total = owned[NZ - 1]
    for k in range(NZ - 1):
        z_copy(k).wait_recv()
        total = total + from_z[k]
    table[mx, whole(mz)] = total

    def g_copy(k):
        spot = table.at[mx, whole(mz)]
        return remote(spot, spot, g_send.at[k], g_recv.at[k], cell(z_of(k), mx), me_g)

    def ag(kind, k):
        z = lax.rem(mz + NZ - z_offset(k), NZ)
        spot, to = (
            (table.at[mx, whole(z)], right),
            (table.at[mx, whole(z)], left),
            (table.at[x_left, top(z)], right),
            (table.at[x_right, low(z)], left),
        )[kind]
        return remote(spot, spot, ag_send.at[kind, k], ag_recv.at[kind, k], to, me_g)

    for k in range(NZ - 1):
        g_copy(k).start()
    order = (7, 5, 6, 3, 4, 1, 2, 0)

    def pass_on(k):
        ag(0, k).wait_recv()
        ag(2, k).start()
        ag(1, k).wait_recv()
        ag(3, k).start()

    for spot, k in enumerate(order):
        if k != NZ - 1:
            g_copy(k).wait_recv()
        ag(0, k).start()
        ag(1, k).start()
        if spot >= 1:
            pass_on(order[spot - 1])

    def column(row):
        return jnp.broadcast_to(row, (LANES, PAD)).T

    counts = jnp.concatenate(
        [table[mx, COUNT_ROW : COUNT_ROW + 1, :], table[mx, COUNT_ROW + 1 : COUNT_ROW + 2, :]], axis=1
    )
    weight = column(counts)
    cols[0] = weight
    cols[1] = 1.0 / weight
    cols[2] = 1.0 / (weight - 1.0)

    def gene_stats(g):
        one, two = table[g, 0:BATCHES, :], table[g, BATCHES:COUNT_ROW, :]
        share = cols[1, 0:BATCHES, :]
        grand = jnp.sum(one, axis=0, keepdims=True) / CELLS
        mean = one * share
        within = two - one * mean
        pooled = jnp.sum(within, axis=0, keepdims=True) / CELLS + 1e-06
        return mean, within, grand, pooled

    mean, within, grand, pooled = gene_stats(mx)
    gamma_hat = (mean - grand) / jnp.sqrt(pooled)
    delta_hat = within * cols[2, 0:BATCHES, :] / pooled
    spare = jnp.zeros((PAD - BATCHES, LANES), f32)

    def over_genes(v):
        return lax.dot_general(
            jnp.ones((8, LANES), f32),
            jnp.concatenate([v, spare], axis=0),
            NT,
            precision=lax.Precision.HIGHEST,
            preferred_element_type=f32,
        )

    sub_wide = lax.broadcasted_iota(i32, (8, PAD), 0)
    t0, t1 = over_genes(gamma_hat), over_genes(gamma_hat * gamma_hat)
    t2, t3 = over_genes(delta_hat), over_genes(delta_hat * delta_hat)
    terms[0] = jnp.where(sub_wide == 0, t0, jnp.where(sub_wide == 1, t1, jnp.where(sub_wide == 2, t2, t3)))

    def terms_over_y(r):
        return remote(
            terms.at[0], terms_y.at[r], t_send.at[0, r], t_recv.at[0, r], me_c, lax.rem(me_g + r, 2 * NY)
        )

    def terms_over_x(r):
        return remote(
            terms.at[1],
            terms_x.at[r],
            t_send.at[1, r],
            t_recv.at[1, r],
            cell(mz, lax.rem(mx + r, NX)),
            me_g,
        )

    for r in range(1, 2 * NY):
        terms_over_y(r).start()
    pass_on(order[-1])
    running = terms[0]
    for r in range(1, 2 * NY):
        terms_over_y(r).wait_recv()
        running = running + terms_y[r]
    terms[1] = running
    for r in range(1, NX):
        terms_over_x(r).start()
    for k in order:
        ag(2, k).wait_recv()
        ag(3, k).wait_recv()
    for g in range(GROUPS):
        mean, within, grand, pooled = gene_stats(g)
        gene_rows[0:1, g * LANES : (g + 1) * LANES] = grand
        gene_rows[1:2, g * LANES : (g + 1) * LANES] = jnp.sqrt(pooled)
        gene_rows[2:3, g * LANES : (g + 1) * LANES] = 1.0 / jnp.sqrt(pooled)
        gene_rows[3:4, g * LANES : (g + 1) * LANES] = 1.0 / pooled
    for r in range(1, NX):
        terms_over_x(r).wait_recv()
        running = running + terms_x[r]
    gamma_bar = running[0:1, :] / GENES
    tau_sq = (running[1:2, :] - GENES * gamma_bar * gamma_bar) / (GENES - 1)
    delta_mean = running[2:3, :] / GENES
    delta_var = (running[3:4, :] - GENES * delta_mean * delta_mean) / (GENES - 1) + 1e-06
    a_prior = (2.0 * delta_var + delta_mean * delta_mean) / delta_var
    b_prior = (delta_mean * delta_var + delta_mean * delta_mean * delta_mean) / delta_var
    cols[3] = column(counts * tau_sq)
    cols[4] = column(gamma_bar)
    cols[5] = column(1.0 / (0.5 * counts + a_prior - 1.0))
    cols[6] = column(b_prior)

    block = 40

    def shrink(i, carry):
        start = pl.multiple_of(i * block, 8)
        rows = pl.ds(start, block)
        weight, share, share_less = cols[0, rows], cols[1, rows], cols[2, rows]
        pull, centre, inverse, prior = cols[3, rows], cols[4, rows], cols[5, rows], cols[6, rows]
        slope = 0.5 * weight * inverse
        hats, leans, floors, deltas = [], [], [], []
        for g in range(GROUPS):
            lanes = slice(g * LANES, (g + 1) * LANES)
            one = table[g, rows, :]
            two = table[g, pl.ds(pl.multiple_of(start + BATCHES, 8), block), :]
            mean = one * share
            hat = (mean - gene_rows[0:1, lanes]) * gene_rows[2:3, lanes]
            delta = (two - one * mean) * share_less * gene_rows[3:4, lanes]
            hats.append(hat)
            leans.append(hat - centre)
            floors.append((0.5 * (weight - 1.0) * delta + prior) * inverse)
            deltas.append(delta)
        moves = [None] * GROUPS
        for _ in range(SWEEPS):
            for g in range(GROUPS):
                moves[g] = deltas[g] * leans[g] / (pull + deltas[g])
                deltas[g] = floors[g] + slope * (moves[g] * moves[g])
        for g in range(GROUPS):
            lanes = slice(g * LANES, (g + 1) * LANES)
            scale = lax.rsqrt(deltas[g])
            wide[0, rows, lanes] = scale * gene_rows[2:3, lanes]
            wide[1, rows, lanes] = (hats[g] - moves[g]) * scale
        return carry

    lax.fori_loop(0, BATCHES // block, shrink, 0)
    wide[:, BATCHES:PAD, :] = jnp.zeros((2, PAD - BATCHES, COLS), f32)
    for g in range(2):
        for side in range(2):
            value = wide[side, :, g * PAD : (g + 1) * PAD]
            upper = value.astype(bf16)
            at = slice((2 * g + side) * PAD, (2 * g + side + 1) * PAD)
            pair[0:PAD, at] = upper
            pair[PAD : 2 * PAD, at] = (value - upper.astype(f32)).astype(bf16)

    other = 1 - mh
    partner = my * 2 + other
    to_right, to_left = y_right * 2 + mh, y_left * 2 + mh
    upper_rows, lower_rows = slice(0, CHUNK_TOP), slice(CHUNK_TOP, COMPONENTS)

    def y_at(i):
        step = jnp.where(i == 0, 2, jnp.where(i == 1, 1, jnp.where(i == 2, 3, 0)))
        return lax.rem(my + step, NY)

    def swap(i):
        return remote(part.at[i], part_recv.at[i], d_send.at[i], d_recv.at[i], me_c, partner)

    def y_copy(kind):
        src, dst, to = (
            (role.at[0, upper_rows], y_via_left, to_right),
            (role.at[0, lower_rows], y_via_right, to_left),
            (role.at[1, lower_rows], y_from_left.at[lower_rows], to_right),
            (role.at[2, upper_rows], y_from_right.at[upper_rows], to_left),
            (role.at[1, upper_rows], y_from_left.at[upper_rows], to_right),
            (role.at[2, lower_rows], y_from_right.at[lower_rows], to_left),
        )[kind]
        return remote(src, dst, y_send.at[kind], y_recv.at[kind], me_c, to)

    def adjust(i, carry):
        mine = i >= NY
        place = jnp.where(mine, i - NY, i)
        chunk = jnp.where(mine, mh, other) * NY + y_at(place)
        rows = pl.ds(pl.multiple_of(chunk * STEP, STEP), STEP)
        members = onehot[rows, :]
        members = jnp.concatenate([members, members], axis=1)
        lows = []
        for g in range(2):
            lanes = slice(g * PAD, (g + 1) * PAD)
            found = jnp.dot(members, pair[:, 2 * g * PAD : 2 * (g + 1) * PAD], preferred_element_type=f32)
            grand, gene_sd = gene_rows[0:1, lanes], gene_rows[1:2, lanes]
            standard = (xv[rows, lanes].astype(f32) - grand) * found[:, :PAD] - found[:, PAD:]
            outv[rows, lanes] = (gene_sd * standard + grand).astype(bf16)
            lows.append(standard.astype(bf16))
        out_copy(i, rows).start()
        part[i] = lax.dot_general(
            loadings_t[...], jnp.concatenate(lows, axis=1), NT, preferred_element_type=f32
        )

        @pl.when(i < NY)
        def _():
            swap(i).start()

        @pl.when(mine)
        def _():
            swap(place).wait_recv()
            role[place] = part[i] + part_recv[place]

        @pl.when(i == NY)
        def _():
            y_copy(0).start()
            y_copy(1).start()

        @pl.when(i == NY + 1)
        def _():
            y_copy(2).start()

        @pl.when(i == NY + 2)
        def _():
            y_copy(3).start()
            y_copy(0).wait_recv()
            role[1, upper_rows] += y_via_left[...]
            y_copy(4).start()
            y_copy(1).wait_recv()
            role[2, lower_rows] += y_via_right[...]
            y_copy(5).start()

        return carry

    def out_copy(i, rows):
        return pltpu.make_async_copy(outv.at[rows, :], adjusted_hbm.at[rows, :], out_sem.at[i])

    lax.fori_loop(0, 2 * NY, adjust, 0)
    for kind in range(2, 6):
        y_copy(kind).wait_recv()
    mine = mh * NY
    final[mine + my] = role[3] + y_from_left[...] + y_from_right[...]

    def y_gather(kind):
        spot, to = (
            (final.at[mine + my, upper_rows], to_right),
            (final.at[mine + my, lower_rows], to_left),
            (final.at[mine + my, lower_rows], to_right),
            (final.at[mine + my, upper_rows], to_left),
            (final.at[mine + y_left, upper_rows], to_right),
            (final.at[mine + y_right, lower_rows], to_left),
        )[kind]
        return remote(spot, spot, y_send.at[6 + kind], y_recv.at[6 + kind], me_c, to)

    def share(i, y):
        spot = final.at[mine + y]
        return remote(spot, spot, d_send.at[NY + i], d_recv.at[NY + i], me_c, partner)

    def store(i, chunk):
        return pltpu.make_async_copy(
            final.at[chunk],
            scores_hbm.at[:, pl.ds(pl.multiple_of(chunk * STEP, STEP), STEP)],
            fin_sem.at[i],
        )

    for kind in range(4):
        y_gather(kind).start()
    share(0, my).start()
    store(0, mine + my).start()
    y_gather(0).wait_recv()
    y_gather(4).start()
    y_gather(1).wait_recv()
    y_gather(5).start()
    y_gather(2).wait_recv()
    share(1, y_left).start()
    store(1, mine + y_left).start()
    y_gather(3).wait_recv()
    share(2, y_right).start()
    store(2, mine + y_right).start()
    y_gather(4).wait_recv()
    y_gather(5).wait_recv()
    share(3, y_opp).start()
    store(3, mine + y_opp).start()
    for i, y in enumerate((my, y_left, y_right, y_opp)):
        share(i, y).wait_recv()
        store(NY + i, other * NY + y).start()

    for k in range(NZ):
        for kind in range(6):
            rs(kind, k).wait_send()
        for kind in range(4):
            ag(kind, k).wait_send()
        if k < NZ - 1:
            z_copy(k).wait_send()
            g_copy(k).wait_send()
    for r in range(1, 2 * NY):
        terms_over_y(r).wait_send()
    for r in range(1, NX):
        terms_over_x(r).wait_send()
    for i in range(NY):
        swap(i).wait_send()
    for kind in range(6):
        y_copy(kind).wait_send()
        y_gather(kind).wait_send()
    for i, y in enumerate((my, y_left, y_right, y_opp)):
        share(i, y).wait_send()
        store(i, mine + y).wait()
        store(NY + i, other * NY + y).wait()
    for i in range(2 * NY):
        out_copy(i, pl.ds(i * STEP, STEP)).wait()


def body(expression, labels, loadings):
    dma = pltpu.SemaphoreType.DMA
    vmem = pltpu.VMEM
    adjusted, scores_t = pl.pallas_call(
        kernel,
        out_shape=(
            jax.ShapeDtypeStruct((ROWS, COLS), bf16),
            jax.ShapeDtypeStruct((COMPONENTS, ROWS), f32),
        ),
        in_specs=[
            pl.BlockSpec(memory_space=vmem),
            pl.BlockSpec(memory_space=pl.ANY),
            pl.BlockSpec(memory_space=vmem),
        ],
        out_specs=(pl.BlockSpec(memory_space=pl.ANY), pl.BlockSpec(memory_space=pl.ANY)),
        scratch_shapes=[
            vmem((ROWS, COLS), bf16),
            vmem((ROWS, COLS), bf16),
            vmem((ROWS, PAD), bf16),
            vmem((208, COLS), f32),
            vmem((208, COLS), f32),
            vmem((8, PAD), f32),
            vmem((GROUPS, STACK, LANES), f32),
            vmem((NZ, HALF, LANES), f32),
            vmem((NZ, PART - HALF, LANES), f32),
            vmem((NZ, PART, LANES), f32),
            vmem((NZ, PART, LANES), f32),
            vmem((NZ, PART, LANES), f32),
            vmem((NZ, PART, LANES), f32),
            vmem((GROUPS, STACK, LANES), f32),
            vmem((2, 8, PAD), f32),
            vmem((2 * NY, 8, PAD), f32),
            vmem((NX, 8, PAD), f32),
            vmem((7, PAD, LANES), f32),
            vmem((8, COLS), f32),
            vmem((2, PAD, COLS), f32),
            vmem((2 * PAD, 2 * COLS), bf16),
            vmem((2 * NY, COMPONENTS, STEP), f32),
            vmem((NY, COMPONENTS, STEP), f32),
            vmem((NY, COMPONENTS, STEP), f32),
            vmem((CHUNK_TOP, STEP), f32),
            vmem((COMPONENTS - CHUNK_TOP, STEP), f32),
            vmem((COMPONENTS, STEP), f32),
            vmem((COMPONENTS, STEP), f32),
            vmem((2 * NY, COMPONENTS, STEP), f32),
            dma((ROWS // READ,)),
            dma((2 * NY,)),
            dma((2 * NY,)),
            dma((6, NZ)),
            dma((6, NZ)),
            dma((NZ - 1,)),
            dma((NZ - 1,)),
            dma((NZ - 1,)),
            dma((NZ - 1,)),
            dma((4, NZ)),
            dma((4, NZ)),
            dma((2, 2 * NY)),
            dma((2, 2 * NY)),
            dma((2 * NY,)),
            dma((2 * NY,)),
            dma((12,)),
            dma((12,)),
        ],
        compiler_params=pltpu.CompilerParams(
            collective_id=0, has_side_effects=True, vmem_limit_bytes=56 * 1024 * 1024
        ),
        name="combat",
    )(labels.reshape(ROWS // LANES, LANES), expression, loadings.T)
    return adjusted, scores_t.T


def solution(mesh):
    return jax.shard_map(
        body,
        mesh=mesh,
        in_specs=(P("cells", "genes"), P("cells"), P("genes", None)),
        out_specs=(P("cells", "genes"), P("cells", None)),
        check_vma=False,
    )
```

time: 251 us -> 88.6 us (0.35)
  blocking collectives: 97.3 us -> 0 us
  Pallas kernels: 0 us -> 81.1 us
  other arithmetic: 39.6 us -> 0 us
  waiting for transfers between devices: 35.6 us -> 0 us
  local copies, waits for them, and re-layouts: 34.8 us -> 5.48 us
  matrix products: 15.2 us -> 0 us
  between operations: 14.2 us -> 0.65 us
  starting transfers between devices: 7.87 us -> 0 us
  loops' own time: 5.7 us -> 0 us
    pallas_call x0 -> x1, Pallas kernels: none -> 81.1 us  [body(): pl.pallas_call(kernel, out_shape=(jax.ShapeDtypeStruct((ROWS, COLS), bf16...]
    all_to_all x4 -> x0, blocking collectives: 80.8 us -> none  [the longest x3 47.2 us: sent_to_all(): lax.all_to_all(jnp.broadcast_to(value[None], (length, *value.shape)), axi...]
    reduce_scatter x1 -> x0, waiting for transfers between devices: 27.2 us -> none  [sum_by_parts_2(): lax.psum_scatter(padded_to(lines, lax.axis_size(axis)), axis, scatter_dim...]
    dynamic_update_slice x8 -> x0, local copies, waits for them, and re-layouts: 17.6 us -> none  [body(): adjusted, partial_value = lax.map(adjust, indices)]
    all_gather x1 -> x0, blocking collectives: 16.5 us -> none  [sum_by_parts_2(): whole = lax.all_gather(own, axis).reshape(-1, *lines.shape[1:])]
    dot_general x20 -> x0, matrix products: 15.2 us -> none  [the longest x4 4.22 us: accumulate(): product = jnp.dot(members, stacked, preferred_element_type=jnp.float32)]
    convert_element_type x15 -> x0, other arithmetic: 12.5 us -> none  [the longest x5 6.88 us: split_three(): upper_part = lax.optimization_barrier(initial.astype(jnp.bfloat16))]
    dynamic_update_slice x4 -> x0, other arithmetic: 11.5 us -> none  [body(): adjusted, partial_value = lax.map(adjust, indices)]
  transfers between devices with their start and end apart: 3 -> 0, of which waited for: 3 -> 0; matrix products, arithmetic and copies ran while one was open for 0% -> 0% of each run, Pallas kernels for 0% -> 0%
where the time goes in v1:
time: 88.6 us; the launch traced here: 87.3 us
  Pallas kernels  81.1 us (92%)
  local copies, waits for them, and re-layouts  5.48 us (6%)
    pallas_call x1, Pallas kernels, body(): pl.pallas_call(kernel, out_shape=(jax.ShapeDtypeStruct((ROWS, COLS), bf16...  81.1 us
    unnamed x4, local copies, waits for them, and re-layouts  5.48 us

profile of v1, /device:TPU:1, one launch (start us, length us, event | category | flops | bytes accessed | tf_op | source)
XLA Modules:
  0.0 87.3 jit_solution(13030827627684608790)
XLA Ops:
  0.6 81.1 %combat.1 = (bf16[4096,512]{1,0:T(8,128)(2,1)}, f32[50,4096]{1,0:T(8,128)}) custom-call(s32[32,128]{1,0:T(8,128)} %bitcast.5, bf16[4096,512]{1,0:T(8,128)(2,1)} %x_hbm.1, bf16[50,512]{1,0:T(8,128)(2,1)} %bitcast.4), custom_call_target="tpu_custom_call" | custom-call | tf_op jit(solution)/shard_map/combat/pallas_call | solution.py:557
  81.8 0.0 copy-start
  81.8 4.6 %copy.7 = bf16[4096,512]{1,0:T(8,128)(2,1)} copy(bf16[4096,512]{1,0:T(8,128)(2,1)} %get-tuple-element.8) | data formatting | bytes 8388608
  86.3 0.0 copy-done
  86.3 0.9 %copy.8 = f32[4096,50]{0,1:T(8,128)} copy(f32[4096,50]{0,1:T(8,128)S(1)} %bitcast.3) | data formatting | bytes 1638400
Async XLA Ops:
  81.8 4.6 %copy-start = (f32[50,4096]{1,0:T(8,128)S(1)}, f32[50,4096]{1,0:T(8,128)}, u32[]{:S(2)}) copy-start(f32[50,4096]{1,0:T(8,128)} %get-tuple-element.5) | copy-start | bytes 2457604

commit v2 on v1

--- a/solution.py
+++ b/solution.py
@@ -25,6 +25,8 @@
 PAD = 256
 READ = 1024
 STEP = 512
+LAG = 3
+GATHER_LAG = 5
 CHUNK_TOP = 32
 
 f32, bf16, i32 = jnp.float32, jnp.bfloat16, jnp.int32
@@ -51,10 +53,9 @@
     labels,
     x_hbm,
     loadings_t,
-    adjusted_hbm,
-    scores_hbm,
+    outv,
+    scores_out,
     xv,
-    outv,
     onehot,
     acc_one,
     acc_two,
@@ -83,8 +84,6 @@
     y_from_right,
     final,
     x_sem,
-    out_sem,
-    fin_sem,
     rs_send,
     rs_recv,
     z_send,
@@ -194,10 +193,6 @@
     def z_copy(k):
         return remote(owned.at[k], from_z.at[k], z_send.at[k], z_recv.at[k], cell(z_of(k), mx), me_g)
 
-    def issue(k):
-        for kind in range(4):
-            rs(kind, k).start()
-
     def merge(k):
         z = z_of(k)
         rs(0, k).wait_recv()
@@ -206,6 +201,8 @@
         rs(1, k).wait_recv()
         sums[x_left, low(z)] += via_right[k]
         rs(5, k).start()
+        rs(2, k).start()
+        rs(3, k).start()
 
     def finish(k):
         for kind in range(2, 6):
@@ -214,25 +211,27 @@
         if k < NZ - 1:
             z_copy(k).start()
 
-    issue(0)
-    issue(1)
+    for k in range(NZ):
+        rs(0, k).start()
+        rs(1, k).start()
 
     def spread_labels(i, carry):
-        wide_labels = jnp.broadcast_to(labels[pl.ds(i, 1), :].astype(f32), (LANES, LANES)).T
+        tile = labels[pl.ds(pl.multiple_of(i * 8, 8), 8), :].astype(f32)
         ids = lax.broadcasted_iota(i32, (LANES, LANES), 1).astype(f32)
-        rows = pl.ds(pl.multiple_of(i * LANES, LANES), LANES)
-        onehot[rows, 0:LANES] = jnp.where(wide_labels == ids, 1.0, 0.0).astype(bf16)
-        onehot[rows, LANES:PAD] = jnp.where(wide_labels == ids + LANES, 1.0, 0.0).astype(bf16)
+        for j in range(8):
+            wide_labels = jnp.broadcast_to(tile[j : j + 1, :], (LANES, LANES)).T
+            rows = pl.ds(pl.multiple_of(i * 8 * LANES + j * LANES, LANES), LANES)
+            onehot[rows, 0:LANES] = jnp.where(wide_labels == ids, 1.0, 0.0).astype(bf16)
+            onehot[rows, LANES:PAD] = jnp.where(wide_labels == ids + LANES, 1.0, 0.0).astype(bf16)
         return carry
 
-    lax.fori_loop(0, ROWS // LANES, spread_labels, 0)
-    for k in range(NZ):
-        merge(k)
-        if k + 2 < NZ:
-            issue(k + 2)
-        if k >= 1:
-            finish(k - 1)
-    finish(NZ - 1)
+    half_labels = ROWS // (16 * LANES)
+    lax.fori_loop(0, half_labels, spread_labels, 0)
+    for k in range(NZ + LAG):
+        if k < NZ:
+            merge(k)
+        if k >= LAG:
+            finish(k - LAG)
     total = owned[NZ - 1]
     for k in range(NZ - 1):
         z_copy(k).wait_recv()
@@ -253,9 +252,9 @@
         )[kind]
         return remote(spot, spot, ag_send.at[kind, k], ag_recv.at[kind, k], to, me_g)
 
-    for k in range(NZ - 1):
+    order = (7, 5, 6, 3, 4, 1, 2, 0)
+    for k in order[1:]:
         g_copy(k).start()
-    order = (7, 5, 6, 3, 4, 1, 2, 0)
 
     def pass_on(k):
         ag(0, k).wait_recv()
@@ -268,8 +267,10 @@
             g_copy(k).wait_recv()
         ag(0, k).start()
         ag(1, k).start()
-        if spot >= 1:
-            pass_on(order[spot - 1])
+        if spot == 0:
+            lax.fori_loop(half_labels, 2 * half_labels, spread_labels, 0)
+        if spot >= GATHER_LAG:
+            pass_on(order[spot - GATHER_LAG])
 
     def column(row):
         return jnp.broadcast_to(row, (LANES, PAD)).T
@@ -327,7 +328,8 @@
 
     for r in range(1, 2 * NY):
         terms_over_y(r).start()
-    pass_on(order[-1])
+    for k in order[NZ - GATHER_LAG :]:
+        pass_on(k)
     running = terms[0]
     for r in range(1, 2 * NY):
         terms_over_y(r).wait_recv()
@@ -438,7 +440,6 @@
             standard = (xv[rows, lanes].astype(f32) - grand) * found[:, :PAD] - found[:, PAD:]
             outv[rows, lanes] = (gene_sd * standard + grand).astype(bf16)
             lows.append(standard.astype(bf16))
-        out_copy(i, rows).start()
         part[i] = lax.dot_general(
             loadings_t[...], jnp.concatenate(lows, axis=1), NT, preferred_element_type=f32
         )
@@ -472,9 +473,6 @@
             y_copy(5).start()
 
         return carry
-
-    def out_copy(i, rows):
-        return pltpu.make_async_copy(outv.at[rows, :], adjusted_hbm.at[rows, :], out_sem.at[i])
 
     lax.fori_loop(0, 2 * NY, adjust, 0)
     for kind in range(2, 6):
@@ -497,34 +495,30 @@
         spot = final.at[mine + y]
         return remote(spot, spot, d_send.at[NY + i], d_recv.at[NY + i], me_c, partner)
 
-    def store(i, chunk):
-        return pltpu.make_async_copy(
-            final.at[chunk],
-            scores_hbm.at[:, pl.ds(pl.multiple_of(chunk * STEP, STEP), STEP)],
-            fin_sem.at[i],
-        )
+    def store(chunk):
+        scores_out[:, pl.ds(pl.multiple_of(chunk * STEP, STEP), STEP)] = final[chunk]
 
     for kind in range(4):
         y_gather(kind).start()
     share(0, my).start()
-    store(0, mine + my).start()
+    store(mine + my)
     y_gather(0).wait_recv()
     y_gather(4).start()
     y_gather(1).wait_recv()
     y_gather(5).start()
     y_gather(2).wait_recv()
     share(1, y_left).start()
-    store(1, mine + y_left).start()
+    store(mine + y_left)
     y_gather(3).wait_recv()
     share(2, y_right).start()
-    store(2, mine + y_right).start()
+    store(mine + y_right)
     y_gather(4).wait_recv()
     y_gather(5).wait_recv()
     share(3, y_opp).start()
-    store(3, mine + y_opp).start()
+    store(mine + y_opp)
     for i, y in enumerate((my, y_left, y_right, y_opp)):
         share(i, y).wait_recv()
-        store(NY + i, other * NY + y).start()
+        store(other * NY + y)
 
     for k in range(NZ):
         for kind in range(6):
@@ -545,10 +539,6 @@
         y_gather(kind).wait_send()
     for i, y in enumerate((my, y_left, y_right, y_opp)):
         share(i, y).wait_send()
-        store(i, mine + y).wait()
-        store(NY + i, other * NY + y).wait()
-    for i in range(2 * NY):
-        out_copy(i, pl.ds(i * STEP, STEP)).wait()
 
 
 def body(expression, labels, loadings):
@@ -557,17 +547,16 @@
     adjusted, scores_t = pl.pallas_call(
         kernel,
         out_shape=(
-            jax.ShapeDtypeStruct((ROWS, COLS), bf16),
-            jax.ShapeDtypeStruct((COMPONENTS, ROWS), f32),
+            pltpu.VMEM((ROWS, COLS), bf16),
+            pltpu.VMEM((COMPONENTS, ROWS), f32),
         ),
         in_specs=[
             pl.BlockSpec(memory_space=vmem),
-            pl.BlockSpec(memory_space=pl.ANY),
+            pl.BlockSpec(memory_space=pltpu.HBM),
             pl.BlockSpec(memory_space=vmem),
         ],
-        out_specs=(pl.BlockSpec(memory_space=pl.ANY), pl.BlockSpec(memory_space=pl.ANY)),
+        out_specs=(pl.BlockSpec(memory_space=vmem), pl.BlockSpec(memory_space=vmem)),
         scratch_shapes=[
-            vmem((ROWS, COLS), bf16),
             vmem((ROWS, COLS), bf16),
             vmem((ROWS, PAD), bf16),
             vmem((208, COLS), f32),
@@ -597,8 +586,6 @@
             vmem((COMPONENTS, STEP), f32),
             vmem((2 * NY, COMPONENTS, STEP), f32),
             dma((ROWS // READ,)),
-            dma((2 * NY,)),
-            dma((2 * NY,)),
             dma((6, NZ)),
             dma((6, NZ)),
             dma((NZ - 1,)),

time: 88.6 us -> 71.9 us (0.81); the launches traced: 87.3 us -> 71.8 us
  Pallas kernels: 81.1 us -> 68.2 us
  local copies, waits for them, and re-layouts: 5.48 us -> 2.94 us
    pallas_call x1, Pallas kernels: 81.1 us -> 68.2 us  [body(): pl.pallas_call(kernel, out_shape=(pltpu.VMEM((ROWS, COLS), bf16), pltpu.V...]
    unnamed x4 -> x2, local copies, waits for them, and re-layouts: 5.48 us -> 2.94 us
where the time goes in v2:
time: 71.9 us; the launch traced here: 71.8 us
  Pallas kernels  68.2 us (95%)
  local copies, waits for them, and re-layouts  2.94 us (4%)
    pallas_call x1, Pallas kernels, body(): pl.pallas_call(kernel, out_shape=(pltpu.VMEM((ROWS, COLS), bf16), pltpu.V...  68.2 us
    unnamed x2, local copies, waits for them, and re-layouts  2.94 us

profile of v2, /device:TPU:1, one launch (start us, length us, event | category | flops | bytes accessed | tf_op | source)
XLA Modules:
  0.0 71.8 jit_solution(5911284668930898535)
XLA Ops:
  0.6 68.2 %combat.1 = (bf16[4096,512]{1,0:T(8,128)(2,1)S(1)}, f32[50,4096]{1,0:T(8,128)S(1)}) custom-call(s32[32,128]{1,0:T(8,128)} %bitcast.5, bf16[4096,512]{1,0:T(8,128)(2,1)} %x_hbm.1, bf16[50,512]{1,0:T(8,128)(2,1)} %bitcast.4), custom_call_target="tpu_custom_call" | custom-call | tf_op jit(solution)/shard_map/combat/pallas_call | solution.py:547
  68.8 2.0 %copy.7 = bf16[4096,512]{1,0:T(8,128)(2,1)} copy(bf16[4096,512]{1,0:T(8,128)(2,1)S(1)} %get-tuple-element.6) | data formatting | bytes 8388608
  70.8 0.9 %copy.8 = f32[4096,50]{0,1:T(8,128)} copy(f32[4096,50]{0,1:T(8,128)S(1)} %bitcast.3) | data formatting | bytes 1638400
